TPU v7x, 128 devices: a whole 4x4x4 slice. The times are simulated.
128 devices in a mesh: rep: 1, data: 16 (over z, y), expert: 8 (over x, core).
Axes of the slice: x: 4, y: 4, z: 4, core: 2. Of those that a mesh axis runs over, the one named last changes fastest.
Arguments:
- x_in: bfloat16 [2, 131072, 768], P(None, ('rep', 'expert', 'data'))
- expert_idx: int32 [2, 131072, 1], P(None, ('rep', 'expert', 'data'))
- gate_wt: float32 [2, 131072, 1], P(None, ('rep', 'expert', 'data'))
- w_gate: bfloat16 [32, 768, 3072], P('expert', 'data')
- w_up: bfloat16 [32, 768, 3072], P('expert', 'data')
- w_down: bfloat16 [32, 3072, 768], P('expert', None, 'data')
Outputs:
- output: bfloat16 [2, 131072, 768], P(None, ('rep', 'expert', 'data'))
All inputs are finite; a program needn't handle non-finite values.
Results may differ from a plain program's by a relative error of at most 0.001.
Values are sent between devices in bfloat16 or wider.
A program may use at most 1 GiB of HBM per device.

v0:
```python
import jax
import jax.numpy as jnp
from jax import lax
from jax.sharding import PartitionSpec as P, NamedSharding


def dispatch_block(x_blk, ids_blk, n_exp, capacity):
    tok_loc, n_top = ids_blk.shape
    pair_count = tok_loc * n_top
    slot_total = n_exp * capacity
    flat_ids = ids_blk.reshape(pair_count)
    one_hot = (flat_ids[:, None] == jnp.arange(n_exp, dtype=jnp.int32)[None, :]).astype(jnp.int32)
    slot_of = jnp.sum((jnp.cumsum(one_hot, axis=0) - one_hot) * one_hot, axis=1)
    is_kept = slot_of < capacity
    dest_pos = jnp.where(is_kept, flat_ids * capacity + slot_of, slot_total)
    source_of = jnp.full((slot_total,), pair_count, jnp.int32).at[dest_pos].set(jnp.arange(pair_count, dtype=jnp.int32), mode='drop')
    tok_of = jnp.minimum(source_of // n_top, tok_loc - 1)
    send_rows = jnp.where((source_of < pair_count)[:, None], jnp.take(x_blk, tok_of, axis=0), jnp.zeros((), x_blk.dtype))
    return send_rows, dest_pos, is_kept


def combine_block(x_blk, gate_blk, back_rows, dest_pos, is_kept):
    tok_loc, n_top = gate_blk.shape
    slot_total = back_rows.shape[0]
    pair_out = jnp.take(back_rows, jnp.minimum(dest_pos, slot_total - 1), axis=0).reshape(tok_loc, n_top, -1)
    weight = jnp.where(is_kept.reshape(tok_loc, n_top), gate_blk, 0.0)
    mix_sum = jnp.sum(pair_out.astype(jnp.float32) * weight[:, :, None], axis=1)
    return (x_blk.astype(jnp.float32) + mix_sum).astype(jnp.bfloat16)


def expert_mlp(rows_in, wg_full, wu_full, wd_full):
    gate_pre = jnp.einsum('lrd,ldf->lrf', rows_in, wg_full, preferred_element_type=jnp.float32)
    up_pre = jnp.einsum('lrd,ldf->lrf', rows_in, wu_full, preferred_element_type=jnp.float32)
    hidden = (jax.nn.silu(gate_pre) * up_pre).astype(jnp.bfloat16)
    return jnp.einsum('lrf,lfd->lrd', hidden, wd_full, preferred_element_type=jnp.float32).astype(jnp.bfloat16)


def solution(mesh):
    expert_devs = mesh.shape['expert']
    row_spec = P(None, ('rep', 'expert', 'data'), None)
    up_spec = P('expert', 'data', None)
    down_spec = P('expert', None, 'data')

    def per_device(x_loc, idx_loc, gate_loc, wg_loc, wu_loc, wd_loc):
        n_loc = wg_loc.shape[0]
        n_exp = n_loc * expert_devs
        d_model = x_loc.shape[2]
        tok_loc = idx_loc.shape[1]
        n_top = idx_loc.shape[2]
        capacity = 8 * ((5 * n_top * tok_loc + 32 * n_exp - 1) // (32 * n_exp))
        wg_full = lax.all_gather(wg_loc, 'data', axis=1, tiled=True)
        wu_full = lax.all_gather(wu_loc, 'data', axis=1, tiled=True)
        wd_full = lax.all_gather(wd_loc, 'data', axis=2, tiled=True)
        results = []
        for mb_index in range(x_loc.shape[0]):
            send_rows, dest_pos, is_kept = dispatch_block(x_loc[mb_index], idx_loc[mb_index], n_exp, capacity)
            recv_rows = lax.all_to_all(send_rows.reshape(expert_devs, n_loc, capacity, d_model), 'expert', 0, 2, tiled=True)
            out_rows = expert_mlp(recv_rows.reshape(n_loc, expert_devs * capacity, d_model), wg_full, wu_full, wd_full)
            back_rows = lax.all_to_all(out_rows.reshape(1, n_loc, expert_devs * capacity, d_model), 'expert', 2, 0, tiled=True)
            results.append(combine_block(x_loc[mb_index], gate_loc[mb_index], back_rows.reshape(n_exp * capacity, d_model), dest_pos, is_kept))
        return jnp.stack(results)

    return jax.shard_map(per_device, mesh=mesh, in_specs=(row_spec, row_spec, row_spec, up_spec, up_spec, down_spec), out_specs=row_spec, check_vma=False)
```

profile of v0, /device:TPU:1, one launch (start us, length us, event | category | flops | bytes accessed | tf_op | source)
XLA Modules:
  0.0 510.1 jit_solution(4076596165498613726)
XLA Ops:
  6.5 0.0 all-gather.4.cloned.1.call-start
  6.5 0.7 all-gather.4.cloned.1.call-update
  7.3 0.0 all-gather.6.cloned.1.call-start
  7.3 0.7 all-gather.6.cloned.1.call-update
  8.0 0.0 all-gather.8.cloned.1.call-start
  8.1 0.7 all-gather.8.cloned.1.call-update
  8.8 9.0 %reduce-window.16 = s32[32,8,128]{2,1,0:T(8,128)S(1)} reduce-window(s32[32,8,128]{2,1,0:T(8,128)S(1)} %fusion.15, s32[]{:T(128)} %constant.58.clone.1), window={size=1x1x128 pad=0_0x0_0x127_0}, to_apply=%region_4.7 | reduce-window | flops 4161536 | bytes 262148 | tf_op jit(solution)/shard_map/reduce-window.2
  17.8 0.1 slice.52
  17.9 0.1 copy.24
  18.1 0.1 copy.25
  18.2 9.0 %reduce-window.14 = s32[32,8,128]{2,1,0:T(8,128)S(1)} reduce-window(s32[32,8,128]{2,1,0:T(8,128)S(1)} %fusion.14, s32[]{:T(128)} %constant.58.clone.1), window={size=1x1x128 pad=0_0x0_0x127_0}, to_apply=%region_0.0 | reduce-window | flops 4161536 | bytes 262148 | tf_op jit(solution)/shard_map/reduce-window
  27.2 0.1 slice.50
  27.3 0.1 copy.19
  27.5 0.1 copy.20
  27.5 0.1 broadcast_add_fusion
  27.7 0.1 broadcast_add_fusion.1
  27.9 4.3 scatter_custom_fusion.1
  32.3 2.1 slice_bitcast_fusion.1
  34.4 4.9 gather_fusion.2
  39.3 3.2 select_select_fusion
  42.5 5.8 %all-to-all-start.2 = ((bf16[8,4,40,768]{3,2,1,0:T(8,128)(2,1)}), bf16[8,4,40,768]{3,2,1,0:T(8,128)(2,1)S(1)}, u32[]{:S(2)}, u32[]{:S(2)}) async-start(bf16[8,4,40,768]{3,2,1,0:T(8,128)(2,1)} %bitcast.26), calls=%async_computation.2 | async-start | bytes 3932160 | tf_op jit(solution)/shard_map/all_to_all | solution.py:57
  48.3 4.3 scatter_custom_fusion
  52.6 4.9 gather_fusion
  57.5 3.1 select_select_fusion.1
  60.7 12.2 %all-to-all-done.2 = bf16[8,4,40,768]{3,2,1,0:T(8,128)(2,1)S(1)} async-done(((bf16[8,4,40,768]{3,2,1,0:T(8,128)(2,1)}), bf16[8,4,40,768]{3,2,1,0:T(8,128)(2,1)S(1)}, u32[]{:S(2)}, u32[]{:S(2)}) %all-to-all-start.2) | async-done | bytes 1966112 | tf_op jit(solution)/shard_map/all_to_all | solution.py:57
  72.9 5.4 %all-to-all-start = ((bf16[8,4,40,768]{3,2,1,0:T(8,128)(2,1)}), bf16[8,4,40,768]{3,2,1,0:T(8,128)(2,1)}, u32[]{:S(2)}, u32[]{:S(2)}) async-start(bf16[8,4,40,768]{3,2,1,0:T(8,128)(2,1)} %bitcast.8), calls=%async_computation | async-start | bytes 3932160 | tf_op jit(solution)/shard_map/all_to_all | solution.py:57
  78.3 1.4 copy.26
  79.7 23.3 %all-to-all-done = bf16[8,4,40,768]{3,2,1,0:T(8,128)(2,1)} async-done(((bf16[8,4,40,768]{3,2,1,0:T(8,128)(2,1)}), bf16[8,4,40,768]{3,2,1,0:T(8,128)(2,1)}, u32[]{:S(2)}, u32[]{:S(2)}) %all-to-all-start) | async-done | bytes 1966112 | tf_op jit(solution)/shard_map/all_to_all | solution.py:57
  103.0 3.1 copy.21
  106.1 28.4 %all-gather.4.cloned.1.call-done = bf16[4,768,3072]{2,1,0:T(8,128)(2,1)} async-done(((bf16[4,48,3072]{2,1,0:T(8,128)(2,1)}), bf16[4,768,3072]{2,1,0:T(8,128)(2,1)}) %all-gather.4.cloned.1.call-update) | async-done | bytes 18874384 | tf_op jit(solution)/shard_map/all_gather | solution.py:51
  134.5 16.0 %fusion.25 = f32[4,320,3072]{2,1,0:T(8,128)} fusion(bf16[4,320,768]{2,1,0:T(8,128)(2,1)S(1)} %bitcast.104, bf16[4,768,3072]{2,1,0:T(8,128)(2,1)} %all-gather.4.cloned.1.call-done), kind=kOutput, calls=%fused_computation.72 | convolution fusion | flops 6039797760 | bytes 36569088 | tf_op jit(solution)/shard_map/lrd,ldf->lrf/dot_general | solution.py:32
  150.5 107.8 %all-gather.6.cloned.1.call-done = bf16[4,768,3072]{2,1,0:T(8,128)(2,1)} async-done(((bf16[4,48,3072]{2,1,0:T(8,128)(2,1)}), bf16[4,768,3072]{2,1,0:T(8,128)(2,1)}) %all-gather.6.cloned.1.call-update) | async-done | bytes 18874384 | tf_op jit(solution)/shard_map/all_gather | solution.py:52
  258.3 123.8 %all-gather.8.cloned.1.call-done = bf16[4,3072,768]{1,2,0:T(8,128)(2,1)} async-done(((bf16[4,3072,48]{1,2,0:T(8,128)(2,1)}), bf16[4,3072,768]{1,2,0:T(8,128)(2,1)}) %all-gather.8.cloned.1.call-update) | async-done | bytes 18874384 | tf_op jit(solution)/shard_map/all_gather | solution.py:53
  382.1 22.1 %convert_bitcast_fusion = bf16[1,4,320,768]{3,2,1,0:T(8,128)(2,1)} fusion(bf16[4,3072,768]{1,2,0:T(8,128)(2,1)} %all-gather.8.cloned.1.call-done, f32[4,320,3072]{2,1,0:T(8,128)} %fusion.25, bf16[4,320,768]{2,1,0:T(8,128)(2,1)S(1)} %bitcast.105, bf16[4,768,3072]{2,1,0:T(8,128)(2,1)} %all-gather.6.cloned.1.call-done), kind=kOutput, calls=%fused_computation.19 | convolution fusion | flops 12104171520 | bytes 57409536 | tf_op jit(solution)/shard_map/lrf,lfd->lrd/dot_general | solution.py:35
  404.1 4.3 copy.27
  408.5 5.2 %all-to-all-start.3 = ((bf16[1,4,320,768]{3,1,0,2:T(4,128)(2,1)}), bf16[1,4,320,768]{3,1,0,2:T(4,128)(2,1)S(1)}, u32[]{:S(2)}, u32[]{:S(2)}) async-start(bf16[1,4,320,768]{3,1,0,2:T(4,128)(2,1)} %copy.27), calls=%async_computation.3 | async-start | bytes 3932160 | tf_op jit(solution)/shard_map/all_to_all | solution.py:59
  413.6 13.9 %fusion.24 = f32[4,320,3072]{2,1,0:T(8,128)} fusion(bf16[4,320,768]{2,1,0:T(8,128)(2,1)} %bitcast.102, bf16[4,768,3072]{2,1,0:T(8,128)(2,1)} %all-gather.4.cloned.1.call-done), kind=kOutput, calls=%fused_computation.71 | convolution fusion | flops 6039797760 | bytes 36569088 | tf_op jit(solution)/shard_map/lrd,ldf->lrf/dot_general | solution.py:32
  427.5 22.4 %convert_bitcast_fusion.1 = bf16[1,4,320,768]{3,2,1,0:T(8,128)(2,1)} fusion(bf16[4,3072,768]{1,2,0:T(8,128)(2,1)} %all-gather.8.cloned.1.call-done, f32[4,320,3072]{2,1,0:T(8,128)} %fusion.24, bf16[4,320,768]{2,1,0:T(8,128)(2,1)} %bitcast.103, bf16[4,768,3072]{2,1,0:T(8,128)(2,1)} %all-gather.6.cloned.1.call-done), kind=kOutput, calls=%fused_computation.20 | convolution fusion | flops 12104171520 | bytes 57409536 | tf_op jit(solution)/shard_map/lrf,lfd->lrd/dot_general | solution.py:35
  449.9 4.4 copy.22
  454.3 0.0 copy-start.12
  454.3 0.0 all-to-all-done.3
  454.3 4.8 all-to-all-start.1
  459.3 1.8 copy.28
  461.1 22.8 %all-to-all-done.1 = bf16[1,4,320,768]{3,1,0,2:T(4,128)(2,1)} async-done(((bf16[1,4,320,768]{3,1,0,2:T(4,128)(2,1)}), bf16[1,4,320,768]{3,1,0,2:T(4,128)(2,1)}, u32[]{:S(2)}, u32[]{:S(2)}) %all-to-all-start.1) | async-done | bytes 1966112 | tf_op jit(solution)/shard_map/all_to_all | solution.py:59
  483.8 3.1 copy.23
  486.9 5.2 %gather_fusion.3 = bf16[1024,768]{1,0:T(8,128)(2,1)} fusion(bf16[1280,768]{1,0:T(8,128)(2,1)S(1)} %bitcast.98, s32[1024]{0:T(1024)S(1)} %broadcast_clamp_fusion), kind=kCustom, calls=%fused_computation.3.clone | custom fusion | bytes 3149824 | tf_op jit(solution)/shard_map/jit(_take)/gather | solution.py:25
  492.1 7.5 %gather_fusion.1 = bf16[1024,768]{1,0:T(8,128)(2,1)} fusion(bf16[1280,768]{1,0:T(8,128)(2,1)} %bitcast.99, s32[1024]{0:T(1024)S(1)} %broadcast_clamp_fusion.1), kind=kCustom, calls=%fused_computation.1.clone | custom fusion | bytes 3149824 | tf_op jit(solution)/shard_map/jit(_take)/gather | solution.py:25
  499.6 3.9 fusion.7
  (49 shorter events, 0.3 us)
Async XLA Ops:
  6.5 2.2 copy-start.11
  6.5 128.0 %all-gather.4.cloned.1.call-start = ((), (), s32[]{:S(2)}) async-start(), calls=%async_computation.4 | async-start | bytes 20054016 | tf_op jit(solution)/shard_map/all_gather | solution.py:51
  7.3 251.1 %all-gather.6.cloned.1.call-start = ((), (), s32[]{:S(2)}) async-start(), calls=%async_computation.5 | async-start | bytes 20054016 | tf_op jit(solution)/shard_map/all_gather | solution.py:52
  8.0 374.1 %all-gather.8.cloned.1.call-start = ((), (), s32[]{:S(2)}) async-start(), calls=%async_computation.6 | async-start | bytes 20054016 | tf_op jit(solution)/shard_map/all_gather | solution.py:53
  8.8 23.5 %copy-start.3 = (s32[1,1024,1]{1,2,0:T(1,128)}, s32[1,1024,1]{1,2,0:T(1,128)S(1)}, u32[]{:S(2)}) copy-start(s32[1,1024,1]{1,2,0:T(1,128)S(1)} %get-tuple-element.17) | copy-start | bytes 12292
  8.8 23.5 %copy-start.5 = (s32[1,1024,1]{1,2,0:T(1,128)}, s32[1,1024,1]{1,2,0:T(1,128)S(1)}, u32[]{:S(2)}) copy-start(s32[1,1024,1]{1,2,0:T(1,128)S(1)} %get-tuple-element.18) | copy-start | bytes 12292
  27.7 4.6 copy-start.7
  27.9 4.4 copy-start.9
  42.5 30.4 %all-to-all-start.2 = ((bf16[8,4,40,768]{3,2,1,0:T(8,128)(2,1)}), bf16[8,4,40,768]{3,2,1,0:T(8,128)(2,1)S(1)}, u32[]{:S(2)}, u32[]{:S(2)}) async-start(bf16[8,4,40,768]{3,2,1,0:T(8,128)(2,1)} %bitcast.26), calls=%async_computation.2 | async-start | bytes 3932160 | tf_op jit(solution)/shard_map/all_to_all | solution.py:57
  72.9 30.2 %all-to-all-start = ((bf16[8,4,40,768]{3,2,1,0:T(8,128)(2,1)}), bf16[8,4,40,768]{3,2,1,0:T(8,128)(2,1)}, u32[]{:S(2)}, u32[]{:S(2)}) async-start(bf16[8,4,40,768]{3,2,1,0:T(8,128)(2,1)} %bitcast.8), calls=%async_computation | async-start | bytes 3932160 | tf_op jit(solution)/shard_map/all_to_all | solution.py:57
  103.0 31.5 %copy-start.2 = (bf16[1,4,8,40,768]{4,3,2,1,0:T(8,128)(2,1)S(1)}, bf16[1,4,8,40,768]{4,3,2,1,0:T(8,128)(2,1)}, u32[]{:S(2)}) copy-start(bf16[1,4,8,40,768]{4,3,2,1,0:T(8,128)(2,1)} %copy.26) | copy-start | bytes 5898244
  408.5 45.8 %all-to-all-start.3 = ((bf16[1,4,320,768]{3,1,0,2:T(4,128)(2,1)}), bf16[1,4,320,768]{3,1,0,2:T(4,128)(2,1)S(1)}, u32[]{:S(2)}, u32[]{:S(2)}) async-start(bf16[1,4,320,768]{3,1,0,2:T(4,128)(2,1)} %copy.27), calls=%async_computation.3 | async-start | bytes 3932160 | tf_op jit(solution)/shard_map/all_to_all | solution.py:59
  454.3 4.9 copy-start.6
  454.3 4.9 copy-start.8
  454.3 4.9 copy-start.4
  454.3 4.9 copy-start.10
  454.3 4.9 copy-start.12
  454.3 4.8 copy-start.1
  454.3 29.5 %all-to-all-start.1 = ((bf16[1,4,320,768]{3,1,0,2:T(4,128)(2,1)}), bf16[1,4,320,768]{3,1,0,2:T(4,128)(2,1)}, u32[]{:S(2)}, u32[]{:S(2)}) async-start(bf16[1,4,320,768]{3,1,0,2:T(4,128)(2,1)} %copy.22), calls=%async_computation.1 | async-start | bytes 3932160 | tf_op jit(solution)/shard_map/all_to_all | solution.py:59
  492.1 7.5 %copy-start = (bf16[2,1024,768]{2,1,0:T(8,128)(2,1)S(1)}, bf16[2,1024,768]{2,1,0:T(8,128)(2,1)}, u32[]{:S(2)}) copy-start(bf16[2,1024,768]{2,1,0:T(8,128)(2,1)} %param.10) | copy-start | bytes 9437188
Sparse Core Ops, SparseCore 0:
  9.5 124.9 all-gather.3
  136.6 121.6 all-gather.5
  260.5 121.5 all-gather.7
where the time goes:
time: 511 us; the launch traced here: 510 us
  waiting for transfers between devices  320 us (63%)
  matrix products  74.3 us (15%)
  local copies, waits for them, and re-layouts  51.9 us (10%)
  other arithmetic  28.8 us (6%)
  starting transfers between devices  21.3 us (4%)
  between operations  13.5 us (3%)
    all_gather x1, waiting for transfers between devices, per_device(): wd_full = lax.all_gather(wd_loc, 'data', axis=2, tiled=True)  124 us
    all_gather x1, waiting for transfers between devices, per_device(): wu_full = lax.all_gather(wu_loc, 'data', axis=1, tiled=True)  108 us
    dot_general x2, matrix products, expert_mlp(): jnp.einsum('lrf,lfd->lrd', hidden, wd_full, preferred_element_type=jnp.fl...  44.5 us
    all_to_all x2, waiting for transfers between devices, per_device(): lax.all_to_all(send_rows.reshape(expert_devs, n_loc, capacity, d_model),...  35.5 us
    dot_general x2, matrix products, expert_mlp(): jnp.einsum('lrd,ldf->lrf', rows_in, wg_full, preferred_element_type=jnp.f...  29.9 us
    all_gather x1, waiting for transfers between devices, per_device(): wg_full = lax.all_gather(wg_loc, 'data', axis=1, tiled=True)  28.4 us
    all_to_all x2, waiting for transfers between devices, per_device(): lax.all_to_all(out_rows.reshape(1, n_loc, expert_devs * capacity, d_model...  22.8 us
    another operation x6, other arithmetic  18.3 us
  transfers between devices with their start and end apart: 7, of which 6 were waited for; matrix products, arithmetic and copies ran while one was open for 21% of the time, Pallas kernels for 0%

commit v1 on v0

v1 whole, which is shorter than its diff:
```python
import functools

import jax
import jax.numpy as jnp
from jax import lax
from jax.experimental import pallas as pl
from jax.experimental.pallas import tpu as pltpu
from jax.sharding import PartitionSpec as P

MESH = pl.DeviceIdType.MESH
N_CHUNK = 3
N_EXP = 32
CAP = 40
ROWS = 2 * CAP
D = 768
FF = 3072
HALF = FF // 2
TOK = 1024
SL = 48


def moe_kernel(x_ref, idx_ref, gate_ref, wg, wu, wd, y_ref,
               W, ST, S, Xr, acc, O, B, dT, gT,
               s1, s2, s3, xs, rs, ss1, ss2, ssx):
    fc = HALF // N_CHUNK
    d = lax.axis_index('data')
    g = lax.axis_index('expert')
    z, y = lax.div(d, 4), lax.rem(d, 4)
    xx, c = lax.div(g, 2), lax.rem(g, 2)
    own_p = lax.div(y, 2)
    yo = 3 - y
    yi = y + 1 - 2 * lax.rem(y, 2)
    sib = 1 - c

    def dev(zv, yv, xv, cv):
        return {'data': zv * 4 + yv, 'expert': xv * 2 + cv}

    def remote(src, dst, send, recv, to):
        return pltpu.make_async_remote_copy(src_ref=src, dst_ref=dst, send_sem=send, recv_sem=recv, device_id=to, device_id_type=MESH)

    def wait_bytes(ref, sem):
        pltpu.make_async_copy(ref, ref, sem).wait()

    bsem = pltpu.get_barrier_semaphore()
    n_peer = 0
    for dx in range(4):
        for dz in range(4):
            for b in range(2):
                if dx or dz or b:
                    pl.semaphore_signal(bsem, inc=1, device_id=dev(lax.rem(z + dz, 4), yo if b else y, lax.rem(xx + dx, 4), c), device_id_type=MESH)
                    n_peer += 1
    for dz in range(4):
        pl.semaphore_signal(bsem, inc=1, device_id=dev(lax.rem(z + dz, 4), y, xx, sib), device_id_type=MESH)
        n_peer += 1
    pl.semaphore_signal(bsem, inc=1, device_id=dev(z, yi, xx, c), device_id_type=MESH)
    n_peer += 1
    pl.semaphore_wait(bsem, n_peer)

    def send_w(j):
        for a in range(2):
            zt = 2 * c + a
            for o in range(2):
                l = 2 * a + (1 - own_p if o else own_p)
                for k in range(2):
                    local = jnp.logical_and(zt == z, c == k)
                    for t, w in enumerate((wg, wu, wd)):
                        src = w.at[l, :, pl.ds(k * HALF + j * fc, fc)]
                        dst = ST.at[j, t, z] if o else W.at[k, j, t, z, y]

                        @pl.when(local)
                        def _():
                            pltpu.make_async_copy(src, dst, s1.at[o, j]).start()

                        @pl.when(jnp.logical_not(local))
                        def _():
                            remote(src, dst, ss1.at[t], s1.at[o, j], dev(zt, y, xx, k)).start()

    def col(j, yv):
        return W.at[c, j, :, :, yv]

    def to_sib(j, yv):
        remote(col(j, yv), col(j, yv), ss2.at[2], s3.at[j], dev(z, y, xx, sib)).start()

    def step_a(j):
        wait_bytes(ST.at[j], s1.at[1, j])
        remote(ST.at[j], col(j, y), ss2.at[0], s2.at[0, j], dev(z, yo, xx, c)).start()
        wait_bytes(col(j, y), s1.at[0, j])
        remote(col(j, y), col(j, y), ss2.at[1], s2.at[1, j], dev(z, yi, xx, c)).start()
        to_sib(j, y)

    def step_b(j):
        wait_bytes(col(j, yo), s2.at[0, j])
        remote(col(j, yo), col(j, yo), ss2.at[1], s2.at[2, j], dev(z, yi, xx, c)).start()
        to_sib(j, yo)

    def step_c(j):
        wait_bytes(col(j, yi), s2.at[1, j])
        to_sib(j, yi)

    def step_d(j):
        wait_bytes(col(j, 3 - yi), s2.at[2, j])
        to_sib(j, 3 - yi)

    def step_e(j):
        wait_bytes(W.at[sib, j], s3.at[j])

    send_w(0)

    earlier = (lax.broadcasted_iota(jnp.int32, (TOK, TOK), 0) < lax.broadcasted_iota(jnp.int32, (TOK, TOK), 1)).astype(jnp.bfloat16)
    dest = []
    for m in range(2):
        ids = idx_ref[m]
        hot = (lax.broadcasted_iota(jnp.int32, (N_EXP, TOK), 0) == ids).astype(jnp.float32)
        before = jnp.dot(hot.astype(jnp.bfloat16), earlier, preferred_element_type=jnp.float32)
        slot = jnp.sum(hot * before, axis=0, keepdims=True)
        kept = slot < CAP
        dest.append(jnp.where(kept, ids.astype(jnp.float32) * CAP + slot, -1.0))
    e_me = 8 * xx + 2 * z + own_p
    for dx in range(4):
        xt = lax.rem(xx + dx, 4)
        parts = []
        for m in range(2):
            pos = (lax.broadcasted_iota(jnp.int32, (8 * CAP, TOK), 0) + xt * (8 * CAP)).astype(jnp.float32)
            pick = (pos == dest[m]).astype(jnp.bfloat16)
            parts.append(jnp.dot(pick, x_ref[m], preferred_element_type=jnp.float32).reshape(8, CAP, D))
        S[pl.ds(xt * 8, 8)] = jnp.concatenate(parts, axis=1).astype(jnp.bfloat16)
        for dz in range(4):
            zt = lax.rem(z + dz, 4)
            for b in range(2):
                yt = yo if b else y
                e = 8 * xt + 2 * zt + lax.div(yt, 2)
                s = (dx * 4 + dz) * 2 + b
                if s == 0:
                    Xr[0] = S[e]
                else:
                    remote(S.at[e], Xr.at[s], ssx.at[0], xs.at[dx], dev(zt, yt, xt, c)).start()
        if dx + 1 < N_CHUNK:
            send_w(dx + 1)
    for j in range(5, N_CHUNK):
        send_w(j)
    for m in range(2):
        dT[m] = jnp.broadcast_to(dest[m], (128, TOK)).T
        gT[m] = jnp.broadcast_to(gate_ref[m], (128, TOK)).T

    def mlp(k, j, r):
        rows = Xr[pl.ds(r * 8, 8)].reshape(8 * ROWS, D)
        gate_pre = jnp.dot(rows, W[k, j, 0].reshape(D, fc), preferred_element_type=jnp.float32)
        up_pre = jnp.dot(rows, W[k, j, 1].reshape(D, fc), preferred_element_type=jnp.float32)
        hidden = (jax.nn.silu(gate_pre) * up_pre).astype(jnp.bfloat16)
        return lax.dot_general(hidden, W[k, j, 2].reshape(D, fc), (((1,), (1,)), ((), ())), preferred_element_type=jnp.float32)

    def wait_rows(r):
        if r == 0:
            wait_bytes(Xr.at[pl.ds(1, 7)], xs.at[0])
        else:
            wait_bytes(Xr.at[pl.ds(r * 8, 8)], xs.at[r])

    step_a(0)
    step_b(0)
    step_c(0)
    for j in range(N_CHUNK):
        if j + 1 < N_CHUNK:
            step_a(j + 1)
        step_d(j)
        if j == 0:
            for r in range(4):
                wait_rows(r)
                acc[r] = mlp(c, 0, r)
        else:
            @pl.loop(0, 4)
            def _(r):
                acc[r] += mlp(c, j, r)
        if j + 1 < N_CHUNK:
            step_b(j + 1)
            step_c(j + 1)
        step_e(j)
        if j + 1 < N_CHUNK:
            @pl.loop(0, 4)
            def _(r):
                acc[r] += mlp(sib, j, r)
    for r in range(4):
        O[pl.ds(r * 8, 8)] = (acc[r] + mlp(sib, N_CHUNK - 1, r)).astype(jnp.bfloat16).reshape(8, ROWS, D)
        for dz in range(4):
            for b in range(2):
                s = (r * 4 + dz) * 2 + b
                if s == 0:
                    B[e_me] = O[0]
                else:
                    remote(O.at[s], B.at[e_me], ssx.at[1], rs.at[r],
                           dev(lax.rem(z + 4 - dz, 4), yo if b else y, lax.rem(xx + 4 - r, 4), c)).start()

    wait_bytes(B.at[pl.ds(0, 7)], rs.at[0])
    for r in range(1, 4):
        wait_bytes(B.at[pl.ds(r * 8, 8)], rs.at[r])
    for m in range(2):
        for q in range(4):
            back = B[pl.ds(q * 8, 8)].astype(jnp.float32)[:, m * CAP:(m + 1) * CAP].reshape(4, ROWS, D)
            Xr[pl.ds(m * 16 + q * 4, 4)] = back.astype(jnp.bfloat16)
    for m in range(2):
        @pl.loop(0, 4)
        def _(i):
            at = pl.ds(pl.multiple_of(i * 256, 256), 256)
            dest_col = dT[m, at]
            pick = jnp.concatenate(
                [(dest_col == (lax.broadcasted_iota(jnp.int32, (256, 128), 1) + 128 * v).astype(jnp.float32)).astype(jnp.bfloat16)
                 for v in range(10)], axis=1)
            back = Xr[pl.ds(m * 16, 16)].reshape(N_EXP * CAP, D)
            mixed = jnp.dot(pick, back, preferred_element_type=jnp.float32)
            weight = jnp.concatenate([gT[m, at]] * (D // 128), axis=1)
            y_ref[m, at] = (x_ref[m, at].astype(jnp.float32) + weight * mixed).astype(jnp.bfloat16)

    has_local = lax.div(z, 2) == c
    for t, w in enumerate((wg, wu, wd)):
        @pl.when(has_local)
        def _():
            wait_bytes(w.at[pl.ds(0, 3)], ss1.at[t])

        @pl.when(jnp.logical_not(has_local))
        def _():
            wait_bytes(w, ss1.at[t])
    wait_bytes(ST, ss2.at[0])
    wait_bytes(W.at[0, :, :, :, pl.ds(0, 2)], ss2.at[1])
    wait_bytes(W.at[0], ss2.at[2])
    wait_bytes(S.at[pl.ds(0, 31)], ssx.at[0])
    wait_bytes(O.at[pl.ds(0, 31)], ssx.at[1])


def solution(mesh):
    row_spec = P(None, ('rep', 'expert', 'data'), None)
    up_spec = P('expert', 'data', None)
    down_spec = P('expert', None, 'data')
    fc = HALF // N_CHUNK
    bf16 = jnp.bfloat16

    def per_device(x_loc, idx_loc, gate_loc, wg_loc, wu_loc, wd_loc):
        vmem = pl.BlockSpec(memory_space=pltpu.VMEM)
        hbm = pl.BlockSpec(memory_space=pl.ANY)
        dma = pltpu.SemaphoreType.DMA
        return pl.pallas_call(
            moe_kernel,
            out_shape=jax.ShapeDtypeStruct((2, TOK, D), bf16),
            in_specs=[vmem, vmem, vmem, hbm, hbm, hbm],
            out_specs=vmem,
            scratch_shapes=[
                pltpu.VMEM((2, N_CHUNK, 3, 4, 4, SL, fc), bf16),
                pltpu.VMEM((N_CHUNK, 3, 4, SL, fc), bf16),
                pltpu.VMEM((N_EXP, ROWS, D), bf16),
                pltpu.VMEM((N_EXP, ROWS, D), bf16),
                pltpu.VMEM((4, 8 * ROWS, D), jnp.float32),
                pltpu.VMEM((N_EXP, ROWS, D), bf16),
                pltpu.VMEM((N_EXP, ROWS, D), bf16),
                pltpu.VMEM((2, TOK, 128), jnp.float32),
                pltpu.VMEM((2, TOK, 128), jnp.float32),
                dma((2, N_CHUNK)), dma((3, N_CHUNK)), dma((N_CHUNK,)), dma((4,)), dma((4,)),
                dma((3,)), dma((3,)), dma((2,)),
            ],
            compiler_params=pltpu.CompilerParams(collective_id=0, has_side_effects=True, vmem_limit_bytes=67043328),
            name='moe',
        )(x_loc, idx_loc.reshape(2, 1, TOK), gate_loc.reshape(2, 1, TOK), wg_loc, wu_loc, wd_loc.transpose(0, 2, 1))

    return jax.shard_map(per_device, mesh=mesh, in_specs=(row_spec, row_spec, row_spec, up_spec, up_spec, down_spec), out_specs=row_spec, check_vma=False)
```

time: 511 us -> 219 us (0.43)
  the two profiles are of different devices: /device:TPU:1 before, /device:TPU:51 now
where the time goes in v1:
time: 219 us
  Pallas kernels  216 us (99%)
  local copies, waits for them, and re-layouts  3.76 us (2%)
    pallas_call x1, Pallas kernels, per_device(): pl.pallas_call(moe_kernel, out_shape=jax.ShapeDtypeStruct((2, TOK, D), bf...  216 us

profile of v1, /device:TPU:51, one launch (start us, length us, event | category | flops | bytes accessed | tf_op | source)
XLA Modules:
  0.0 219.3 jit_solution(14429738555821129248)
XLA Ops:
  0.0 215.5 %moe.1 = bf16[2,1024,768]{2,1,0:T(8,128)(2,1)} custom-call(bf16[2,1024,768]{2,1,0:T(8,128)(2,1)} %x_ref.1, s32[2,1,1024]{2,1,0:T(1,128)} %bitcast.4, f32[2,1,1024]{2,1,0:T(1,128)} %bitcast.5, bf16[4,48,3072]{2,1,0:T(8,128)(2,1)} %wg.1, bf16[4,48,3072]{2,1,0:T(8,128)(2,1)} %wu.1, bf16[4,48,3072]{2,1,0:T(8,128)(2,1)} %bitcast.3), custom_call_target="tpu_custom_call" | custom-call | tf_op jit(solution)/shard_map/moe/pallas_call | solution.py:239
  215.5 3.8 %copy.8 = bf16[2,1024,768]{2,1,0:T(8,128)(2,1)} copy(bf16[2,1024,768]{2,1,0:T(8,128)(2,1)} %moe.1) | data formatting | bytes 6291456

commit v2 on v1

v2 whole, which is shorter than its diff:
```python
import functools

import jax
import jax.numpy as jnp
from jax import lax
from jax.experimental import pallas as pl
from jax.experimental.pallas import tpu as pltpu
from jax.sharding import PartitionSpec as P

MESH = pl.DeviceIdType.MESH
N_CHUNK = 6
N_EXP = 32
CAP = 40
ROWS = 2 * CAP
D = 768
ZY = ((0, 0), (2, 1), (1, 0), (3, 1), (3, 0), (1, 1), (0, 1), (2, 0))
HEAD = ('W0', 'W1', 'W2', 'W3', 'W4', 'W5')
SCHED = (
    'P0', 'X0', 'P1', 'X1', 'A0', 'P2', 'X2', 'A1', 'P3', 'X3', 'Z', 'C0', 'B0', 'A2', 'C1', 'B1', 'A3', 'U0', 'D0',
    'B2', 'A4', 'U1', 'C2', 'B3', 'A5', 'U2', 'E0', 'D1', 'B4', 'U3', 'C3', 'B5', 'R0', 'K0101', 'E1', 'K1201', 'D2',
    'C4', 'E2', 'K2301', 'D3', 'C5', 'E3', 'K3401', 'D4', 'E4', 'K4501', 'R1', 'K0212', 'D5', 'R2', 'R3', 'E5',
)
DONE = (5, 2, 0, 0)
FF = 3072
HALF = FF // 2
TOK = 1024
SL = 48


def moe_kernel(x_ref, idx_ref, gate_ref, wg, wu, wd, y_ref,
               W, ST, S, T1, R1, Xr, acc, B, dT, gT,
               s1, s2, s3, xs1, xs2, rs1, rs2, ss1, ss2, ssx):
    fc = HALF // N_CHUNK
    d = lax.axis_index('data')
    g = lax.axis_index('expert')
    z, y = lax.div(d, 4), lax.rem(d, 4)
    xx, c = lax.div(g, 2), lax.rem(g, 2)
    own_p = lax.div(y, 2)
    yo = 3 - y
    yi = y + 1 - 2 * lax.rem(y, 2)
    sib = 1 - c

    def dev(zv, yv, xv, cv):
        return {'data': zv * 4 + yv, 'expert': xv * 2 + cv}

    def remote(src, dst, send, recv, to):
        return pltpu.make_async_remote_copy(src_ref=src, dst_ref=dst, send_sem=send, recv_sem=recv, device_id=to, device_id_type=MESH)

    def wait_bytes(ref, sem):
        pltpu.make_async_copy(ref, ref, sem).wait()

    bsem = pltpu.get_barrier_semaphore()
    n_peer = 10
    for dx in range(1, 4):
        pl.semaphore_signal(bsem, inc=1, device_id=dev(z, y, lax.rem(xx + dx, 4), c), device_id_type=MESH)
    for dz, b in ZY[1:]:
        pl.semaphore_signal(bsem, inc=1, device_id=dev(lax.rem(z + dz, 4), yo if b else y, xx, c), device_id_type=MESH)
    for dz in range(4):
        pl.semaphore_signal(bsem, inc=1, device_id=dev(lax.rem(z + dz, 4), y, xx, sib), device_id_type=MESH)
        n_peer += 1
    pl.semaphore_signal(bsem, inc=1, device_id=dev(z, yi, xx, c), device_id_type=MESH)
    n_peer += 1
    pl.semaphore_wait(bsem, n_peer)

    def send_w(j):
        for a in range(2):
            zt = 2 * c + a
            for o in range(2):
                l = 2 * a + (1 - own_p if o else own_p)
                for k in range(2):
                    local = jnp.logical_and(zt == z, c == k)
                    for t, w in enumerate((wg, wu, wd)):
                        src = w.at[l, :, pl.ds(k * HALF + j * fc, fc)]
                        dst = ST.at[j, t, z] if o else W.at[k, j, t, z, y]

                        @pl.when(local)
                        def _():
                            pltpu.make_async_copy(src, dst, s1.at[o, j]).start()

                        @pl.when(jnp.logical_not(local))
                        def _():
                            remote(src, dst, ss1.at[t], s1.at[o, j], dev(zt, y, xx, k)).start()

    def col(j, yv):
        return W.at[c, j, :, :, yv]

    def to_sib(j, yv):
        remote(col(j, yv), col(j, yv), ss2.at[2], s3.at[j], dev(z, y, xx, sib)).start()

    def step_a(j):
        wait_bytes(ST.at[j], s1.at[1, j])
        remote(ST.at[j], col(j, y), ss2.at[0], s2.at[0, j], dev(z, yo, xx, c)).start()
        wait_bytes(col(j, y), s1.at[0, j])
        remote(col(j, y), col(j, y), ss2.at[1], s2.at[1, j], dev(z, yi, xx, c)).start()
        to_sib(j, y)

    def step_b(j):
        wait_bytes(col(j, yo), s2.at[0, j])
        remote(col(j, yo), col(j, yo), ss2.at[1], s2.at[2, j], dev(z, yi, xx, c)).start()
        to_sib(j, yo)

    def step_c(j):
        wait_bytes(col(j, yi), s2.at[1, j])
        to_sib(j, yi)

    def step_d(j):
        wait_bytes(col(j, 3 - yi), s2.at[2, j])
        to_sib(j, 3 - yi)

    def step_e(j):
        wait_bytes(W.at[sib, j], s3.at[j])

    ops = dict(W=send_w, A=step_a, B=step_b, C=step_c, D=step_d, E=step_e)

    def run(plan):
        for word in plan:
            ops[word[0]](*[int(v) for v in word[1:]])

    run(HEAD)

    earlier = (lax.broadcasted_iota(jnp.int32, (TOK, TOK), 0) < lax.broadcasted_iota(jnp.int32, (TOK, TOK), 1)).astype(jnp.bfloat16)
    dest = []
    for m in range(2):
        e = idx_ref[m]
        step_x = lax.bitwise_and(lax.shift_right_logical(e, 3) - xx, 3)
        step_z = lax.bitwise_and(lax.shift_right_logical(e, 1) - z, 3)
        other = lax.bitwise_and(e + own_p, 1)
        ids = step_x
        for zb, (dz, b) in enumerate(ZY):
            ids = ids + jnp.where(step_z * 2 + other == dz * 2 + b, 4 * zb, 0)
        hot = (lax.broadcasted_iota(jnp.int32, (N_EXP, TOK), 0) == ids).astype(jnp.float32)
        before = jnp.dot(hot.astype(jnp.bfloat16), earlier, preferred_element_type=jnp.float32)
        slot = jnp.sum(hot * before, axis=0, keepdims=True)
        kept = slot < CAP
        dest.append(jnp.where(kept, ids.astype(jnp.float32) * CAP + slot, -1.0))
    def prep(i):
        parts = []
        for m in range(2):
            pos = (lax.broadcasted_iota(jnp.int32, (8 * CAP, TOK), 0) + i * (8 * CAP)).astype(jnp.float32)
            pick = (pos == dest[m]).astype(jnp.bfloat16)
            parts.append(jnp.dot(pick, x_ref[m], preferred_element_type=jnp.float32).reshape(8, CAP, D))
        rows = jnp.concatenate(parts, axis=1).astype(jnp.bfloat16).reshape(2, 4, ROWS, D)
        S[pl.ds(2 * i, 2)] = rows
        if i:
            T1[pl.ds(2 * i, 2), 0] = rows[:, 0]
        else:
            Xr[0, 0] = rows[0, 0]
            T1[1, 0] = rows[1, 0]

    def send_x(i):
        for zb in (2 * i, 2 * i + 1):
            for dx in (1, 3, 2):
                land = T1 if zb else Xr
                remote(S.at[zb, dx], land.at[zb, dx], ssx.at[0], xs1.at[i], dev(z, y, lax.rem(xx + dx, 4), c)).start()

    def send_zy(i):
        wait_bytes(T1.at[pl.ds(0, 2), pl.ds(0, 3)], xs1.at[i])
        for zb in (2 * i, 2 * i + 1):
            if zb:
                remote(T1.at[zb], Xr.at[zb], ssx.at[1], xs2.at[zb], dev(lax.rem(z + ZY[zb][0], 4), yo if ZY[zb][1] else y, xx, c)).start()

    def columns():
        for m in range(2):
            dT[m] = jnp.broadcast_to(dest[m], (128, TOK)).T
            gT[m] = jnp.broadcast_to(gate_ref[m], (128, TOK)).T

        @pl.loop(0, 4)
        def _(r):
            acc[pl.ds(2 * r, 2)] = jnp.zeros((2, 4 * ROWS, D), jnp.float32)

    def mlp(k, j, r):
        rows = Xr[pl.ds(r * 2, 2)].reshape(8 * ROWS, D)
        gate_pre = jnp.dot(rows, W[k, j, 0].reshape(D, fc), preferred_element_type=jnp.float32)
        up_pre = jnp.dot(rows, W[k, j, 1].reshape(D, fc), preferred_element_type=jnp.float32)
        hidden = (jax.nn.silu(gate_pre) * up_pre).astype(jnp.bfloat16)
        return lax.dot_general(hidden, W[k, j, 2].reshape(D, fc), (((1,), (1,)), ((), ())), preferred_element_type=jnp.float32)

    def wait_rows(r):
        for zb in (2 * r, 2 * r + 1):
            if zb:
                wait_bytes(Xr.at[zb], xs2.at[zb])

    def add(r, value):
        acc[pl.ds(2 * r, 2)] += value.reshape(2, 4 * ROWS, D)

    def work(j0, j1, r0, r1):
        nr = r1 - r0

        @pl.loop(0, 2 * (j1 - j0) * nr)
        def _(i):
            r = r0 + lax.rem(i, nr)
            q = lax.div(i, nr)
            add(r, mlp(lax.rem(q, 2), j0 + lax.div(q, 2), r))

    ops.update(P=prep, X=send_x, U=send_zy, Z=columns, R=wait_rows, K=work)
    run(SCHED)
    wait_bytes(S.at[:, pl.ds(0, 3)], ssx.at[0])
    wait_bytes(T1.at[pl.ds(0, 7)], ssx.at[1])

    def back_x(zb):
        if zb:
            wait_bytes(R1.at[zb], rs1.at[zb])
        for dx in (1, 3, 2):
            remote(R1.at[zb, dx], B.at[zb, dx], ssx.at[3], rs2.at[zb], dev(z, y, lax.rem(xx + 4 - dx, 4), c)).start()
        B[zb, 0] = R1[zb, 0]

    def halves(h0, h1, r):
        if h1 > h0:
            @pl.loop(h0, h1)
            def _(h):
                add(r, mlp(lax.bitwise_and(c + h, 1), lax.div(h, 2), r))

    pending = []
    for r in range(4):
        halves(2 * DONE[r], 2 * N_CHUNK - 1, r)
        total = acc[pl.ds(2 * r, 2)].reshape(8 * ROWS, D) + mlp(sib, N_CHUNK - 1, r)
        S[pl.ds(2 * r, 2)] = total.astype(jnp.bfloat16).reshape(2, 4, ROWS, D)
        if r == 0:
            R1[0] = S[0]
        for zb in (2 * r, 2 * r + 1):
            if zb:
                remote(S.at[zb], R1.at[zb], ssx.at[2], rs1.at[zb],
                       dev(lax.rem(z + 4 - ZY[zb][0], 4), yo if ZY[zb][1] else y, xx, c)).start()
        for zb in pending:
            back_x(zb)
        pending = [2 * r, 2 * r + 1]

    def combine(half, first):
        for zb in half:
            wait_bytes(B.at[zb, pl.ds(1, 3)], rs2.at[zb])
        lo = min(half) // 4
        for m in range(2):
            for q in range(2):
                back = B[pl.ds(lo * 4 + q * 2, 2)].reshape(8, ROWS, D).astype(jnp.float32)[:, m * CAP:(m + 1) * CAP].reshape(4, ROWS, D)
                Xr[m * 2 + q] = back.astype(jnp.bfloat16)

        @pl.loop(0, 8)
        def _(n):
            m, i = lax.div(n, 4), lax.rem(n, 4)
            at = pl.ds(pl.multiple_of(i * 256, 256), 256)
            dest_col = dT[m, at]
            pick = jnp.concatenate(
                [(dest_col == (lax.broadcasted_iota(jnp.int32, (256, 128), 1) + 128 * (v + 5 * lo)).astype(jnp.float32)).astype(jnp.bfloat16)
                 for v in range(5)], axis=1)
            back = Xr[pl.ds(m * 2, 2)].reshape(N_EXP * CAP // 2, D)
            mixed = jnp.dot(pick, back, preferred_element_type=jnp.float32)
            if first:
                acc[n, pl.ds(0, 256)] = mixed
            else:
                weight = jnp.concatenate([gT[m, at]] * (D // 128), axis=1)
                y_ref[m, at] = (x_ref[m, at].astype(jnp.float32) + weight * (acc[n, pl.ds(0, 256)] + mixed)).astype(jnp.bfloat16)

    combine((0, 1, 2, 3), True)
    for zb in pending:
        back_x(zb)
    combine((4, 5, 6, 7), False)

    has_local = lax.div(z, 2) == c
    for t, w in enumerate((wg, wu, wd)):
        @pl.when(has_local)
        def _():
            wait_bytes(w.at[pl.ds(0, 3)], ss1.at[t])

        @pl.when(jnp.logical_not(has_local))
        def _():
            wait_bytes(w, ss1.at[t])
    wait_bytes(ST, ss2.at[0])
    wait_bytes(W.at[0, :, :, :, pl.ds(0, 2)], ss2.at[1])
    wait_bytes(W.at[0], ss2.at[2])
    wait_bytes(S.at[pl.ds(0, 7)], ssx.at[2])
    wait_bytes(R1.at[:, pl.ds(0, 3)], ssx.at[3])


def solution(mesh):
    row_spec = P(None, ('rep', 'expert', 'data'), None)
    up_spec = P('expert', 'data', None)
    down_spec = P('expert', None, 'data')
    fc = HALF // N_CHUNK
    bf16 = jnp.bfloat16

    def per_device(x_loc, idx_loc, gate_loc, wg_loc, wu_loc, wd_loc):
        vmem = pl.BlockSpec(memory_space=pltpu.VMEM)
        hbm = pl.BlockSpec(memory_space=pl.ANY)
        dma = pltpu.SemaphoreType.DMA
        return pl.pallas_call(
            moe_kernel,
            out_shape=jax.ShapeDtypeStruct((2, TOK, D), bf16),
            in_specs=[vmem, vmem, vmem, hbm, hbm, hbm],
            out_specs=vmem,
            scratch_shapes=[
                pltpu.VMEM((2, N_CHUNK, 3, 4, 4, SL, fc), bf16),
                pltpu.VMEM((N_CHUNK, 3, 4, SL, fc), bf16),
                pltpu.VMEM((8, 4, ROWS, D), bf16),
                pltpu.VMEM((8, 4, ROWS, D), bf16),
                pltpu.VMEM((8, 4, ROWS, D), bf16),
                pltpu.VMEM((8, 4, ROWS, D), bf16),
                pltpu.VMEM((8, 4 * ROWS, D), jnp.float32),
                pltpu.VMEM((8, 4, ROWS, D), bf16),
                pltpu.VMEM((2, TOK, 128), jnp.float32),
                pltpu.VMEM((2, TOK, 128), jnp.float32),
                dma((2, N_CHUNK)), dma((3, N_CHUNK)), dma((N_CHUNK,)), dma((4,)), dma((8,)), dma((8,)), dma((8,)),
                dma((3,)), dma((3,)), dma((4,)),
            ],
            compiler_params=pltpu.CompilerParams(collective_id=0, has_side_effects=True, vmem_limit_bytes=67043328),
            name='moe',
        )(x_loc, idx_loc.reshape(2, 1, TOK), gate_loc.reshape(2, 1, TOK), wg_loc, wu_loc, wd_loc.transpose(0, 2, 1))

    return jax.shard_map(per_device, mesh=mesh, in_specs=(row_spec, row_spec, row_spec, up_spec, up_spec, down_spec), out_specs=row_spec, check_vma=False)
```

time: 219 us -> 177 us (0.81)
  the two profiles are of different devices: /device:TPU:51 before, /device:TPU:1 now
where the time goes in v2:
time: 177 us
  Pallas kernels  173 us (98%)
  local copies, waits for them, and re-layouts  3.76 us (2%)
    pallas_call x1, Pallas kernels, per_device(): pl.pallas_call(moe_kernel, out_shape=jax.ShapeDtypeStruct((2, TOK, D), bf...  173 us
    unnamed x1, local copies, waits for them, and re-layouts  3.76 us

profile of v2, /device:TPU:1, one launch (start us, length us, event | category | flops | bytes accessed | tf_op | source)
XLA Modules:
  0.0 177.0 jit_solution(800616398773545958)
XLA Ops:
  0.0 173.3 %moe.1 = bf16[2,1024,768]{2,1,0:T(8,128)(2,1)} custom-call(bf16[2,1024,768]{2,1,0:T(8,128)(2,1)} %x_ref.1, s32[2,1,1024]{2,1,0:T(1,128)} %bitcast.4, f32[2,1,1024]{2,1,0:T(1,128)} %bitcast.5, bf16[4,48,3072]{2,1,0:T(8,128)(2,1)} %wg.1, bf16[4,48,3072]{2,1,0:T(8,128)(2,1)} %wu.1, bf16[4,48,3072]{2,1,0:T(8,128)(2,1)} %bitcast.3), custom_call_target="tpu_custom_call" | custom-call | tf_op jit(solution)/shard_map/moe/pallas_call | solution.py:285
  173.3 3.8 %copy.8 = bf16[2,1024,768]{2,1,0:T(8,128)(2,1)} copy(bf16[2,1024,768]{2,1,0:T(8,128)(2,1)} %moe.1) | data formatting | bytes 6291456

commit v3 on v2

--- a/solution.py
+++ b/solution.py
@@ -28,8 +28,8 @@
 
 
 def moe_kernel(x_ref, idx_ref, gate_ref, wg, wu, wd, y_ref,
-               W, ST, S, T1, R1, Xr, acc, B, dT, gT,
-               s1, s2, s3, xs1, xs2, rs1, rs2, ss1, ss2, ssx):
+               W, ST, S, T1, Xr, acc, B, dT, gT,
+               s1, s2, s3, xs1, xs2, rs, ss1, ss2, ssx):
     fc = HALF // N_CHUNK
     d = lax.axis_index('data')
     g = lax.axis_index('expert')
@@ -50,11 +50,11 @@
         pltpu.make_async_copy(ref, ref, sem).wait()
 
     bsem = pltpu.get_barrier_semaphore()
-    n_peer = 10
-    for dx in range(1, 4):
-        pl.semaphore_signal(bsem, inc=1, device_id=dev(z, y, lax.rem(xx + dx, 4), c), device_id_type=MESH)
-    for dz, b in ZY[1:]:
-        pl.semaphore_signal(bsem, inc=1, device_id=dev(lax.rem(z + dz, 4), yo if b else y, xx, c), device_id_type=MESH)
+    n_peer = 4 * len(ZY) - 1
+    for zb, (dz, b) in enumerate(ZY):
+        for dx in range(4):
+            if zb or dx:
+                pl.semaphore_signal(bsem, inc=1, device_id=dev(lax.rem(z + dz, 4), yo if b else y, lax.rem(xx + dx, 4), c), device_id_type=MESH)
     for dz in range(4):
         pl.semaphore_signal(bsem, inc=1, device_id=dev(lax.rem(z + dz, 4), y, xx, sib), device_id_type=MESH)
         n_peer += 1
@@ -197,37 +197,27 @@
     wait_bytes(S.at[:, pl.ds(0, 3)], ssx.at[0])
     wait_bytes(T1.at[pl.ds(0, 7)], ssx.at[1])
 
-    def back_x(zb):
-        if zb:
-            wait_bytes(R1.at[zb], rs1.at[zb])
-        for dx in (1, 3, 2):
-            remote(R1.at[zb, dx], B.at[zb, dx], ssx.at[3], rs2.at[zb], dev(z, y, lax.rem(xx + 4 - dx, 4), c)).start()
-        B[zb, 0] = R1[zb, 0]
-
     def halves(h0, h1, r):
         if h1 > h0:
             @pl.loop(h0, h1)
             def _(h):
                 add(r, mlp(lax.bitwise_and(c + h, 1), lax.div(h, 2), r))
 
-    pending = []
     for r in range(4):
         halves(2 * DONE[r], 2 * N_CHUNK - 1, r)
         total = acc[pl.ds(2 * r, 2)].reshape(8 * ROWS, D) + mlp(sib, N_CHUNK - 1, r)
         S[pl.ds(2 * r, 2)] = total.astype(jnp.bfloat16).reshape(2, 4, ROWS, D)
-        if r == 0:
-            R1[0] = S[0]
         for zb in (2 * r, 2 * r + 1):
-            if zb:
-                remote(S.at[zb], R1.at[zb], ssx.at[2], rs1.at[zb],
-                       dev(lax.rem(z + 4 - ZY[zb][0], 4), yo if ZY[zb][1] else y, xx, c)).start()
-        for zb in pending:
-            back_x(zb)
-        pending = [2 * r, 2 * r + 1]
+            z_to, y_to = lax.rem(z + 4 - ZY[zb][0], 4), yo if ZY[zb][1] else y
+            for dx in (2, 1, 3, 0):
+                if zb or dx:
+                    remote(S.at[zb, dx], B.at[zb, dx], ssx.at[2 if zb else 3], rs.at[zb], dev(z_to, y_to, lax.rem(xx + 4 - dx, 4), c)).start()
+                else:
+                    B[0, 0] = S[0, 0]
 
     def combine(half, first):
         for zb in half:
-            wait_bytes(B.at[zb, pl.ds(1, 3)], rs2.at[zb])
+            wait_bytes(B.at[zb] if zb else B.at[0, pl.ds(1, 3)], rs.at[zb])
         lo = min(half) // 4
         for m in range(2):
             for q in range(2):
@@ -251,8 +241,6 @@
                 y_ref[m, at] = (x_ref[m, at].astype(jnp.float32) + weight * (acc[n, pl.ds(0, 256)] + mixed)).astype(jnp.bfloat16)
 
     combine((0, 1, 2, 3), True)
-    for zb in pending:
-        back_x(zb)
     combine((4, 5, 6, 7), False)
 
     has_local = lax.div(z, 2) == c
@@ -267,8 +255,8 @@
     wait_bytes(ST, ss2.at[0])
     wait_bytes(W.at[0, :, :, :, pl.ds(0, 2)], ss2.at[1])
     wait_bytes(W.at[0], ss2.at[2])
-    wait_bytes(S.at[pl.ds(0, 7)], ssx.at[2])
-    wait_bytes(R1.at[:, pl.ds(0, 3)], ssx.at[3])
+    wait_bytes(S.at[pl.ds(1, 7)], ssx.at[2])
+    wait_bytes(S.at[0, pl.ds(1, 3)], ssx.at[3])
 
 
 def solution(mesh):
@@ -293,12 +281,11 @@
                 pltpu.VMEM((8, 4, ROWS, D), bf16),
                 pltpu.VMEM((8, 4, ROWS, D), bf16),
                 pltpu.VMEM((8, 4, ROWS, D), bf16),
-                pltpu.VMEM((8, 4, ROWS, D), bf16),
                 pltpu.VMEM((8, 4 * ROWS, D), jnp.float32),
                 pltpu.VMEM((8, 4, ROWS, D), bf16),
                 pltpu.VMEM((2, TOK, 128), jnp.float32),
                 pltpu.VMEM((2, TOK, 128), jnp.float32),
-                dma((2, N_CHUNK)), dma((3, N_CHUNK)), dma((N_CHUNK,)), dma((4,)), dma((8,)), dma((8,)), dma((8,)),
+                dma((2, N_CHUNK)), dma((3, N_CHUNK)), dma((N_CHUNK,)), dma((4,)), dma((8,)), dma((8,)),
                 dma((3,)), dma((3,)), dma((4,)),
             ],
             compiler_params=pltpu.CompilerParams(collective_id=0, has_side_effects=True, vmem_limit_bytes=67043328),

time: 177 us -> 170 us (0.960)
  Pallas kernels: 173 us -> 165 us
    pallas_call x1, Pallas kernels: 173 us -> 165 us  [per_device(): pl.pallas_call(moe_kernel, out_shape=jax.ShapeDtypeStruct((2, TOK, D), bf...]
where the time goes in v3:
time: 170 us; the launch traced here: 169 us
  Pallas kernels  165 us (97%)
  local copies, waits for them, and re-layouts  3.76 us (2%)
    pallas_call x1, Pallas kernels, per_device(): pl.pallas_call(moe_kernel, out_shape=jax.ShapeDtypeStruct((2, TOK, D), bf...  165 us
    unnamed x1, local copies, waits for them, and re-layouts  3.76 us

profile of v3, /device:TPU:1, one launch (start us, length us, event | category | flops | bytes accessed | tf_op | source)
XLA Modules:
  0.0 169.3 jit_solution(2165465463294381613)
XLA Ops:
  0.0 165.5 %moe.1 = bf16[2,1024,768]{2,1,0:T(8,128)(2,1)} custom-call(bf16[2,1024,768]{2,1,0:T(8,128)(2,1)} %x_ref.1, s32[2,1,1024]{2,1,0:T(1,128)} %bitcast.4, f32[2,1,1024]{2,1,0:T(1,128)} %bitcast.5, bf16[4,48,3072]{2,1,0:T(8,128)(2,1)} %wg.1, bf16[4,48,3072]{2,1,0:T(8,128)(2,1)} %wu.1, bf16[4,48,3072]{2,1,0:T(8,128)(2,1)} %bitcast.3), custom_call_target="tpu_custom_call" | custom-call | tf_op jit(solution)/shard_map/moe/pallas_call | solution.py:273
  165.5 3.8 %copy.8 = bf16[2,1024,768]{2,1,0:T(8,128)(2,1)} copy(bf16[2,1024,768]{2,1,0:T(8,128)(2,1)} %moe.1) | data formatting | bytes 6291456

commit v4 on v3

--- a/solution.py
+++ b/solution.py
@@ -16,8 +16,8 @@
 ZY = ((0, 0), (2, 1), (1, 0), (3, 1), (3, 0), (1, 1), (0, 1), (2, 0))
 HEAD = ('W0', 'W1', 'W2', 'W3', 'W4', 'W5')
 SCHED = (
-    'P0', 'X0', 'P1', 'X1', 'A0', 'P2', 'X2', 'A1', 'P3', 'X3', 'Z', 'C0', 'B0', 'A2', 'C1', 'B1', 'A3', 'U0', 'D0',
-    'B2', 'A4', 'U1', 'C2', 'B3', 'A5', 'U2', 'E0', 'D1', 'B4', 'U3', 'C3', 'B5', 'R0', 'K0101', 'E1', 'K1201', 'D2',
+    'P0', 'X0', 'P1', 'X1', 'A0', 'P2', 'X2', 'A1', 'P3', 'X3', 'Z', 'C0', 'B0', 'A2', 'C1', 'B1', 'A3', 'D0', 'B2',
+    'U0', 'A4', 'C2', 'B3', 'U1', 'A5', 'E0', 'D1', 'B4', 'U2', 'C3', 'B5', 'U3', 'R0', 'K0101', 'E1', 'K1201', 'D2',
     'C4', 'E2', 'K2301', 'D3', 'C5', 'E3', 'K3401', 'D4', 'E4', 'K4501', 'R1', 'K0212', 'D5', 'R2', 'R3', 'E5',
 )
 DONE = (5, 2, 0, 0)

time: 170 us -> 171 us (level)
  Pallas kernels: 165 us -> 167 us
    pallas_call x1, Pallas kernels: 165 us -> 167 us  [per_device(): pl.pallas_call(moe_kernel, out_shape=jax.ShapeDtypeStruct((2, TOK, D), bf...]
where the time goes in v4:
time: 171 us
  Pallas kernels  167 us (98%)
  local copies, waits for them, and re-layouts  3.76 us (2%)
    pallas_call x1, Pallas kernels, per_device(): pl.pallas_call(moe_kernel, out_shape=jax.ShapeDtypeStruct((2, TOK, D), bf...  167 us
    unnamed x1, local copies, waits for them, and re-layouts  3.76 us

profile of v4, /device:TPU:1, one launch (start us, length us, event | category | flops | bytes accessed | tf_op | source)
XLA Modules:
  0.0 171.1 jit_solution(4899062112738519938)
XLA Ops:
  0.0 167.4 %moe.1 = bf16[2,1024,768]{2,1,0:T(8,128)(2,1)} custom-call(bf16[2,1024,768]{2,1,0:T(8,128)(2,1)} %x_ref.1, s32[2,1,1024]{2,1,0:T(1,128)} %bitcast.4, f32[2,1,1024]{2,1,0:T(1,128)} %bitcast.5, bf16[4,48,3072]{2,1,0:T(8,128)(2,1)} %wg.1, bf16[4,48,3072]{2,1,0:T(8,128)(2,1)} %wu.1, bf16[4,48,3072]{2,1,0:T(8,128)(2,1)} %bitcast.3), custom_call_target="tpu_custom_call" | custom-call | tf_op jit(solution)/shard_map/moe/pallas_call | solution.py:273
  167.4 3.8 %copy.8 = bf16[2,1024,768]{2,1,0:T(8,128)(2,1)} copy(bf16[2,1024,768]{2,1,0:T(8,128)(2,1)} %moe.1) | data formatting | bytes 6291456
